TPU v7x, 32 devices: a whole 2x2x4 slice. The times are simulated.
32 devices in a mesh: dp: 4 (over x, core), context: 2 (over y), tensor: 4 (over z).
Axes of the slice: x: 2, y: 2, z: 4, core: 2. Of those that a mesh axis runs over, the one named last changes fastest.
Arguments:
- tokens: bfloat16 [12, 512, 1536], P('dp', 'context')
- cotangent: bfloat16 [12, 512, 1536], P('dp', 'context'), may hold values from -6 to 6
- segments: int32 [12, 512], P('dp'), may hold values from 0 to 3, as said below
- positions: int32 [12, 512], P('dp', 'context'), may hold values from 0 to 255, as said below
- norm_attn: bfloat16 [1536], replicated, may hold values from 0.099609375 to 1.8984375
- w_query: bfloat16 [1536, 1536], P(None, 'tensor')
- key_weight: bfloat16 [1536, 768], P(None, 'tensor')
- value_weight: bfloat16 [1536, 768], P(None, 'tensor'), may hold values from -0.15625 to 0.15625
- w_out: bfloat16 [1536, 1536], P('tensor'), may hold values from -0.875 to 0.875
- norm_ffn: bfloat16 [1536], replicated, may hold values from 0.099609375 to 1.8984375
- w_gate: bfloat16 [1536, 4096], P(None, 'tensor'), may hold values from -0.15625 to 0.15625
- w_up: bfloat16 [1536, 4096], P(None, 'tensor'), may hold values from -0.15625 to 0.15625
- w_down: bfloat16 [4096, 1536], P('tensor'), may hold values from -0.09375 to 0.09375
Outputs:
- block_out: bfloat16 [12, 512, 1536], P('dp', 'context')
- input_grad: bfloat16 [12, 512, 1536], P('dp', 'context')
- attn_gain_grad: float32 [1536], replicated
- query_grad: float32 [1536, 1536], P(None, 'tensor')
- key_grad: float32 [1536, 768], P(None, 'tensor')
- value_grad: float32 [1536, 768], P(None, 'tensor')
- out_grad: float32 [1536, 1536], P('tensor')
- ffn_gain_grad: float32 [1536], replicated
- gate_grad: float32 [1536, 4096], P(None, 'tensor')
- up_grad: float32 [1536, 4096], P(None, 'tensor')
- down_grad: float32 [4096, 1536], P('tensor')
Inputs may be any that keep to these rules, and one draw needn't show every extreme that they name: `segments`: each sequence holds exactly four documents, numbered from 0 on its first token, never falling and rising by one at the first token of each further document; one of the four is 256 tokens long and the others are shorter. `positions`: each token's position is its offset from the first token of its document in its sequence.
All inputs are finite; a program needn't handle non-finite values.
Results may differ from a plain program's by a relative error of at most 0.019.
Values may be sent and summed in bfloat16 or wider, within the bound.
A program may use at most 192 MiB of HBM per device.

v0:
```python
import math
import jax
import jax.numpy as jnp
from jax import lax
from jax.sharding import PartitionSpec as P

HEAD_SIZE = 96
EPS = 1e-05
THETA = 100000.0
NEG_LARGE = -1e30


def shifted(x, axis, by):
    peers = lax.axis_size(axis)
    pairs = [(i, i + by) for i in range(peers) if 0 <= i + by < peers]
    return lax.ppermute(x, axis, pairs)


def rope_tables(position_rows):
    steps_half = jnp.arange(HEAD_SIZE // 2).astype(jnp.float32)
    inverse = THETA ** (-2.0 * steps_half / HEAD_SIZE)
    angles = position_rows.astype(jnp.float32)[..., None] * inverse
    return (jnp.cos(angles), jnp.sin(angles))


def apply_rotary(operand, cosine, sine_part):
    half_width = operand.shape[-1] // 2
    lead_half = operand[..., :half_width]
    tail_half = operand[..., half_width:]
    return jnp.concatenate(
        [lead_half * cosine - tail_half * sine_part, tail_half * cosine + lead_half * sine_part],
        axis=-1,
    )


def inverse_rotary(operand, cosine, sine_part):
    half_width = operand.shape[-1] // 2
    lead_half = operand[..., :half_width]
    tail_half = operand[..., half_width:]
    return jnp.concatenate(
        [lead_half * cosine + tail_half * sine_part, tail_half * cosine - lead_half * sine_part],
        axis=-1,
    )


def dot_wide(left_side, right_side):
    return jnp.dot(left_side, right_side, preferred_element_type=jnp.float32)


def on_device(
    tokens,
    cotangent,
    segments,
    positions,
    norm_attn,
    w_query,
    key_weight,
    value_weight,
    w_out,
    norm_ffn,
    w_gate,
    w_up,
    w_down,
):
    single_float = jnp.float32
    brain_float_half = jnp.bfloat16
    seq_count, slice_len, model_width = tokens.shape
    seq_length = segments.shape[1]
    row_count = seq_count * slice_len
    query_width = w_query.shape[1]
    pair_width = key_weight.shape[1]
    kv_heads = pair_width // HEAD_SIZE
    group_of_head = query_width // HEAD_SIZE // kv_heads
    key_block = min(512, seq_length)
    score_scale = 1.0 / math.sqrt(HEAD_SIZE)
    my_slice = lax.axis_index("context")
    first_row = my_slice * slice_len
    query_seg = lax.dynamic_slice_in_dim(segments, first_row, slice_len, 1)
    query_index = first_row + jnp.arange(slice_len, dtype=jnp.int32)
    block_count = (first_row + slice_len + key_block - 1) // key_block
    tok_flat = tokens.reshape(row_count, model_width).astype(single_float)
    inv_attn = lax.rsqrt(jnp.mean(tok_flat * tok_flat, axis=-1, keepdims=True) + EPS)
    normalized_attention_input = (tok_flat * inv_attn * norm_attn.astype(single_float)).astype(
        brain_float_half
    )
    cosine, sine_part = rope_tables(positions)
    cos_query = cosine[:, :, None, None, :]
    sin_query = sine_part[:, :, None, None, :]
    cos_key = cosine[:, :, None, :]
    sin_key = sine_part[:, :, None, :]
    query_rows = apply_rotary(
        dot_wide(normalized_attention_input, w_query).reshape(
            seq_count, slice_len, kv_heads, group_of_head, HEAD_SIZE
        ),
        cos_query,
        sin_query,
    ).astype(brain_float_half)
    keys_local = apply_rotary(
        dot_wide(normalized_attention_input, key_weight).reshape(
            seq_count, slice_len, kv_heads, HEAD_SIZE
        ),
        cos_key,
        sin_key,
    ).astype(brain_float_half)
    values_local = dot_wide(normalized_attention_input, value_weight).astype(brain_float_half)
    pair_local = jnp.concatenate(
        [
            keys_local.reshape(seq_count, slice_len, pair_width),
            values_local.reshape(seq_count, slice_len, pair_width),
        ],
        axis=-1,
    )
    pair_all = lax.all_gather(pair_local, "context", axis=1, tiled=True)

    def score_block(pair_source, start_key):
        piece = lax.dynamic_slice_in_dim(pair_source, start_key, key_block, 1)
        key_part = piece[..., :pair_width].reshape(seq_count, key_block, kv_heads, HEAD_SIZE)
        value_part = piece[..., pair_width:].reshape(seq_count, key_block, kv_heads, HEAD_SIZE)
        scores = (
            jnp.einsum(
                "sigrd,sjgd->sgrij", query_rows, key_part, preferred_element_type=single_float
            )
            * score_scale
        )
        key_seg = lax.dynamic_slice_in_dim(segments, start_key, key_block, 1)
        key_index = start_key + jnp.arange(key_block, dtype=jnp.int32)
        allowed = (key_seg[:, None, :] == query_seg[:, :, None]) & (
            key_index[None, None, :] <= query_index[None, :, None]
        )
        return (scores, allowed[:, None, None, :, :], key_part, value_part)

    def stats_step(index_block, carry):
        run_max, run_sum = carry
        scores, allowed, key_part, value_part = score_block(pair_all, index_block * key_block)
        masked = jnp.where(allowed, scores, NEG_LARGE)
        new_max = jnp.maximum(run_max, jnp.max(masked, axis=-1))
        block_sum = jnp.sum(jnp.where(allowed, jnp.exp(masked - new_max[..., None]), 0.0), axis=-1)
        return (new_max, run_sum * jnp.exp(run_max - new_max) + block_sum)

    stat_shape = (seq_count, kv_heads, group_of_head, slice_len)
    run_max, run_sum = lax.fori_loop(
        0,
        block_count,
        stats_step,
        (jnp.full(stat_shape, NEG_LARGE, single_float), jnp.zeros(stat_shape, single_float)),
    )
    log_total = run_max + jnp.log(run_sum)

    def output_step(index_block, accum):
        scores, allowed, key_part, value_part = score_block(pair_all, index_block * key_block)
        probs = jnp.where(allowed, jnp.exp(scores - log_total[..., None]), 0.0).astype(
            brain_float_half
        )
        return accum + jnp.einsum(
            "sgrij,sjgd->sigrd", probs, value_part, preferred_element_type=single_float
        )

    attn_accum = lax.fori_loop(
        0,
        block_count,
        output_step,
        jnp.zeros((seq_count, slice_len, kv_heads, group_of_head, HEAD_SIZE), single_float),
    )
    attended = attn_accum.astype(brain_float_half).reshape(row_count, query_width)
    attn_total = lax.psum(dot_wide(attended, w_out).astype(jnp.bfloat16), "tensor").astype(
        jnp.float32
    )
    hidden_res = tok_flat + attn_total
    inv_ffn = lax.rsqrt(jnp.mean(hidden_res * hidden_res, axis=-1, keepdims=True) + EPS)
    normed_ffn = (hidden_res * inv_ffn * norm_ffn.astype(single_float)).astype(brain_float_half)
    gate_proj = dot_wide(normed_ffn, w_gate)
    up_proj = dot_wide(normed_ffn, w_up)
    sigmoid_gate = jax.nn.sigmoid(gate_proj)
    silu_gate = gate_proj * sigmoid_gate
    activated = (silu_gate * up_proj).astype(brain_float_half)
    ffn_total = lax.psum(dot_wide(activated, w_down).astype(jnp.bfloat16), "tensor").astype(
        jnp.float32
    )
    block_out = (
        (hidden_res + ffn_total).astype(brain_float_half).reshape(seq_count, slice_len, model_width)
    )
    grad_rows = cotangent.reshape(row_count, model_width)
    down_grad = dot_wide(activated.T, grad_rows)
    grad_act = dot_wide(grad_rows, w_down.T)
    grad_gate = (
        grad_act * up_proj * sigmoid_gate * (1.0 + gate_proj * (1.0 - sigmoid_gate))
    ).astype(brain_float_half)
    grad_up = (grad_act * silu_gate).astype(brain_float_half)
    gate_grad = dot_wide(normed_ffn.T, grad_gate)
    up_grad = dot_wide(normed_ffn.T, grad_up)
    grad_normed_ffn = lax.psum(
        (dot_wide(grad_gate, w_gate.T) + dot_wide(grad_up, w_up.T)).astype(jnp.bfloat16), "tensor"
    ).astype(jnp.float32)
    ffn_gain_grad = jnp.sum(grad_normed_ffn * hidden_res * inv_ffn, axis=0)
    scaled_ffn = grad_normed_ffn * norm_ffn.astype(single_float)
    grad_hidden = (
        grad_rows.astype(single_float)
        + inv_ffn * scaled_ffn
        - hidden_res * inv_ffn**3 * jnp.mean(scaled_ffn * hidden_res, axis=-1, keepdims=True)
    )
    grad_hidden_b = grad_hidden.astype(brain_float_half)
    out_grad = dot_wide(attended.T, grad_hidden_b)
    attended_gradient = (
        dot_wide(grad_hidden_b, w_out.T)
        .astype(brain_float_half)
        .reshape(seq_count, slice_len, kv_heads, group_of_head, HEAD_SIZE)
    )
    attended_heads = attended.reshape(seq_count, slice_len, kv_heads, group_of_head, HEAD_SIZE)
    row_delta = jnp.sum(
        attended_gradient.astype(single_float) * attended_heads.astype(single_float), axis=-1
    )
    delta_heads = jnp.transpose(row_delta, (0, 2, 3, 1))

    def grad_step(index_block, carry):
        query_accum, pair_accum = carry
        start_key = index_block * key_block
        scores, allowed, key_part, value_part = score_block(pair_all, start_key)
        weights = jnp.where(allowed, jnp.exp(scores - log_total[..., None]), 0.0)
        prob_grad = jnp.einsum(
            "sigrd,sjgd->sgrij", attended_gradient, value_part, preferred_element_type=single_float
        )
        score_grad = (weights * (prob_grad - delta_heads[..., None]) * score_scale).astype(
            brain_float_half
        )
        query_accum = query_accum + jnp.einsum(
            "sgrij,sjgd->sigrd", score_grad, key_part, preferred_element_type=single_float
        )
        key_term = jnp.einsum(
            "sgrij,sigrd->sjgd", score_grad, query_rows, preferred_element_type=single_float
        )
        value_term = jnp.einsum(
            "sgrij,sigrd->sjgd",
            weights.astype(brain_float_half),
            attended_gradient,
            preferred_element_type=single_float,
        )
        both_terms = jnp.concatenate(
            [
                key_term.reshape(seq_count, key_block, pair_width),
                value_term.reshape(seq_count, key_block, pair_width),
            ],
            axis=-1,
        )
        current = lax.dynamic_slice_in_dim(pair_accum, start_key, key_block, 1)
        pair_accum = lax.dynamic_update_slice_in_dim(pair_accum, current + both_terms, start_key, 1)
        return (query_accum, pair_accum)

    query_accum, pair_accum = lax.fori_loop(
        0,
        block_count,
        grad_step,
        (
            jnp.zeros((seq_count, slice_len, kv_heads, group_of_head, HEAD_SIZE), single_float),
            jnp.zeros((seq_count, seq_length, 2 * pair_width), single_float),
        ),
    )
    slice_count = lax.axis_size("context")

    def owner_step(turn, incoming):
        owner = my_slice + turn - (slice_count - 1)
        own_rows = lax.dynamic_slice_in_dim(
            pair_accum, jnp.maximum(owner, 0) * slice_len, slice_len, 1
        )
        message = jnp.where(owner >= 0, incoming + own_rows, 0.0)
        return shifted(message, "context", -1)

    arrived = lax.fori_loop(
        0,
        slice_count - 1,
        owner_step,
        jnp.zeros((seq_count, slice_len, 2 * pair_width), single_float),
    )
    pair_grad = arrived + lax.dynamic_slice_in_dim(pair_accum, first_row, slice_len, 1)
    key_linear = (
        inverse_rotary(
            pair_grad[..., :pair_width].reshape(seq_count, slice_len, kv_heads, HEAD_SIZE),
            cos_key,
            sin_key,
        )
        .astype(brain_float_half)
        .reshape(row_count, pair_width)
    )
    value_linear = (
        pair_grad[..., pair_width:].astype(brain_float_half).reshape(row_count, pair_width)
    )
    query_lin = (
        inverse_rotary(query_accum, cos_query, sin_query)
        .astype(brain_float_half)
        .reshape(row_count, query_width)
    )
    query_grad = dot_wide(normalized_attention_input.T, query_lin)
    key_grad = dot_wide(normalized_attention_input.T, key_linear)
    value_grad = dot_wide(normalized_attention_input.T, value_linear)
    back_attn = (
        dot_wide(query_lin, w_query.T)
        + dot_wide(key_linear, key_weight.T)
        + dot_wide(value_linear, value_weight.T)
    )
    grad_normed_attn = lax.psum(back_attn.astype(jnp.bfloat16), "tensor").astype(jnp.float32)
    attn_gain_grad = jnp.sum(grad_normed_attn * tok_flat * inv_attn, axis=0)
    scaled_attn = grad_normed_attn * norm_attn.astype(single_float)
    input_grad = (
        grad_hidden
        + inv_attn * scaled_attn
        - tok_flat * inv_attn**3 * jnp.mean(scaled_attn * tok_flat, axis=-1, keepdims=True)
    )
    input_grad = input_grad.astype(brain_float_half).reshape(seq_count, slice_len, model_width)
    all_sums = lax.psum(
        (
            attn_gain_grad,
            query_grad,
            key_grad,
            value_grad,
            out_grad,
            ffn_gain_grad,
            gate_grad,
            up_grad,
            down_grad,
        ),
        ("dp", "context"),
    )
    return (
        block_out,
        input_grad,
        all_sums[0],
        all_sums[1],
        all_sums[2],
        all_sums[3],
        all_sums[4],
        all_sums[5],
        all_sums[6],
        all_sums[7],
        all_sums[8],
    )


def solution(mesh):
    placed = (
        P("dp", "context", None),
        P("dp", "context", None),
        P("dp", None),
        P("dp", "context"),
        P(),
        P(None, "tensor"),
        P(None, "tensor"),
        P(None, "tensor"),
        P("tensor", None),
        P(),
        P(None, "tensor"),
        P(None, "tensor"),
        P("tensor", None),
    )
    return jax.shard_map(
        on_device,
        mesh=mesh,
        in_specs=placed,
        out_specs=(
            P("dp", "context", None),
            P("dp", "context", None),
            P(),
            P(None, "tensor"),
            P(None, "tensor"),
            P(None, "tensor"),
            P("tensor", None),
            P(),
            P(None, "tensor"),
            P(None, "tensor"),
            P("tensor", None),
        ),
        check_vma=False,
    )
```

profile of v0, /device:TPU:0, one launch (start us, length us, event | category | flops | bytes accessed | tf_op | source)
XLA Modules:
  0.0 889.8 jit_solution(11171474708792457560)
XLA Ops:
  8.1 2.3 fusion.50
  10.4 2.3 fusion.52
  16.5 1.6 convolution_convert_fusion.3
  18.2 1.8 reshape.331
  20.0 2.5 pad_maximum_fusion
  22.6 2.4 copy.51
  25.0 3.1 fusion.57
  29.1 23.4 %all-gather.2.cloned.1.call-done = bf16[3,512,384]{1,0,2:T(4,128)(2,1)} async-done(((bf16[3,256,384]{1,0,2:T(4,128)(2,1)}), bf16[3,512,384]{1,0,2:T(4,128)(2,1)}) %all-gather.2.cloned.1.call-update) | async-done | bytes 1179664 | tf_op jit(solution)/shard_map/all_gather | solution.py:113
  52.6 2.7 copy.53
  55.3 5.6 while.42
  56.9 2.3 fusion.157
  59.3 1.6 select_reduce_fusion.2
  62.6 7.8 while.43
  63.1 2.4 fusion.162
  65.5 4.7 fusion.163
  70.4 3.3 copy.54
  73.7 3.3 reshape.332
  77.0 4.2 convolution_convert_fusion.1
  81.9 94.1 %all-reduce.8.cloned.1.call-done = bf16[768,1536]{1,0:T(8,128)(2,1)} async-done(((bf16[768,1536]{1,0:T(8,128)(2,1)}), bf16[768,1536]{1,0:T(8,128)(2,1)}) %all-reduce.8.cloned.1.call-update) | async-done | bytes 2359312 | tf_op jit(solution)/shard_map/psum | solution.py:165
  176.0 3.4 multiply_reduce_fusion
  181.7 2.6 fusion.70
  184.4 2.6 fusion.69
  187.1 5.0 multiply_convert_fusion.1
  192.0 2.6 fusion.71
  194.7 4.0 add_convert_fusion.1
  198.9 93.6 %all-reduce.10.cloned.1.call-done = bf16[768,1536]{1,0:T(8,128)(2,1)} async-done(((bf16[768,1536]{1,0:T(8,128)(2,1)}), bf16[768,1536]{1,0:T(8,128)(2,1)}) %all-reduce.10.cloned.1.call-update) | async-done | bytes 2359312 | tf_op jit(solution)/shard_map/psum | solution.py:191
  292.5 5.0 fusion.47
  297.7 3.5 fusion.44
  301.2 2.1 copy-done.8
  303.3 2.2 convolution_convert_fusion.2
  305.5 3.7 reshape.335
  309.2 4.4 multiply_reduce_fusion.1
  313.6 3.0 copy.56
  319.1 1.7 broadcast_in_dim.84
  320.8 12.2 %while.44 = (s32[]{:T(128)}, f32[3,256,2,2,96]{1,4,3,2,0:T(8,128)}, f32[3,512,384]{1,2,0:T(8,128)}, s32[]{:T(128)}, s32[3,512]{1,0:T(4,128)S(1)}, /*index=5*/s32...) while((s32[]{:T(128)}, f32[3,256,2,2,96]{1,4,3,2,0:T(8,128)}, ...), condition=%wide.region_14.15_spmd.clone, body=%wide.region_13.14_spmd.clone.sunk | while | flops 1529643776 | bytes 81120576 | solution.py:248
  324.1 1.4 fusion.178
  325.6 2.5 fusion.176
  331.6 1.4 copy-done.6
  333.0 2.5 dynamic-slice_select_fusion
  336.8 3.8 convolution_convert_fusion
  341.7 3.0 copy.58
  344.7 3.3 convert_element_type.180
  348.0 3.0 fusion.72
  351.0 14.2 %collective-permute-done = f32[3,256,384]{1,2,0:T(8,128)} collective-permute-done((f32[3,256,384]{1,2,0:T(8,128)}, f32[3,256,384]{1,2,0:T(8,128)}, u32[]{:S(2)}, u32[]{:S(2)}) %collective-permute-start) | collective-permute-done | bytes 1179680 | tf_op jit(solution)/shard_map/while/body/eval_jaxpr/ppermute | solution.py:16
  365.2 1.5 dynamic-slice_add_fusion
  369.3 2.2 add_convert_fusion
  371.8 7.6 fusion.77
  379.5 4.6 fusion.76
  384.1 4.6 fusion.75
  388.6 2.8 fusion.74
  391.5 2.6 fusion.61
  394.1 1.6 convolution_bitcast_fusion.1
  395.7 1.6 fusion.78
  398.0 144.0 %all-reduce.14.cloned.1.call-done = (bf16[768,1536]{1,0:T(8,128)(2,1)}, bf16[768,1536]{1,0:T(8,128)(2,1)}) async-done(((bf16[768,1536]{1,0:T(8,128)(2,1)}, bf16[768,1536]{1,0:T(8,128)(2,1)}), (bf16[768,1536]{1,0:T(8,128)(2,1)}, bf16[768,1536]{1,0:T(8,128)(2,1)})) %all-reduce.14.cloned.1.call-update) | async-done | bytes 4718608 | tf_op jit(solution)/shard_map/psum | solution.py:176
  542.0 4.1 fusion.49
  546.1 25.9 %all-reduce = (f32[1536]{0:T(1024)}, f32[1536]{0:T(1024)}) all-reduce(f32[1536]{0:T(1024)S(1)} %get-tuple-element.347, f32[1536]{0:T(1024)S(1)} %get-tuple-element.345), channel_id=1, replica_groups=mesh['dp'=4,'context'=2,'tensor'=4] {'dp','context'}, use_global_device_ids=true, to_apply=%region_18.19 | all-reduce | flops 3072 | bytes 24576 | tf_op jit(solution)/shard_map/psum | solution.py:308
  572.0 8.9 %fusion.41 = (bf16[768,1536]{1,0:T(8,128)(2,1)}, bf16[768,1536]{1,0:T(8,128)(2,1)}) fusion(f32[768,1536]{1,0:T(8,128)} %copy-done.8, bf16[768,1536]{1,0:T(8,128)(2,1)} %get-tuple-element.419, bf16[3,256,1536]{2,1,0:T(8,128)(2,1)} %param.19, f32[768]{0:T(1024)S(1)} %broadcast_multiply_fusion, f32[768]{0:T(1024)S(1)} %multiply_multiply_fusion, ...), kind=kLoop, calls=%fused_computation.55 | loop fusion | flops 16515072 | bytes 18889728 | tf_op jit(solution)/shard_map/convert_element_type | solution.py:307
  581.0 282.7 %all-reduce.12.cloned.1.call-done = (f32[1536,384]{1,0:T(8,128)}, f32[1536,192]{0,1:T(8,128)}, f32[1536,192]{0,1:T(8,128)}, f32[384,1536]{1,0:T(8,128)}, f32[153...) async-done(((f32[1536,384]{1,0:T(8,128)}, f32[1536,192]{0,1:T(8,128)}, f32[1536,192]{0,1:T(8,128)}, f32[384,1536]{1,0:T(8,128)}, f32[1536,1024]{1,0:T(8,128)}, ...) | async-done | bytes 25952272 | tf_op jit(solution)/shard_map/psum | solution.py:308
  863.6 3.4 copy.112
  869.3 1.4 copy.115
  870.7 1.6 copy-done.17
  872.4 3.2 copy.116
  875.8 3.2 copy.117
  880.4 2.7 copy.118
  (188 shorter events, 31.9 us)
Async XLA Ops:
  7.2 179.9 %copy-start = (bf16[1024,1536]{1,0:T(8,128)(2,1)S(1)}, bf16[1024,1536]{1,0:T(8,128)(2,1)}, u32[]{:S(2)}) copy-start(bf16[1024,1536]{1,0:T(8,128)(2,1)} %param.31) | copy-start | bytes 9437188
  7.2 3.2 copy-start.44
  7.2 45.4 %all-gather.2.cloned.1.call-start = ((), (), s32[]{:S(2)}) async-start(), calls=%async_computation | async-start | bytes 2359296 | tf_op jit(solution)/shard_map/all_gather | solution.py:113
  10.4 5.1 copy-start.41
  10.4 5.1 copy-start.39
  10.4 3.0 copy-start.26
  12.8 1.7 copy-start.14
  13.4 14.7 %copy-start.21 = (f32[3,256,48]{1,2,0:T(8,128)}, f32[3,256,48]{1,2,0:T(8,128)S(1)}, u32[]{:S(2)}) copy-start(f32[3,256,48]{1,2,0:T(8,128)S(1)} %get-tuple-element.439) | copy-start | bytes 442372
  13.4 14.7 %copy-start.23 = (f32[3,256,48]{1,2,0:T(8,128)}, f32[3,256,48]{1,2,0:T(8,128)S(1)}, u32[]{:S(2)}) copy-start(f32[3,256,48]{1,2,0:T(8,128)S(1)} %get-tuple-element.440) | copy-start | bytes 442372
  13.4 2.1 copy-start.1
  15.5 1.1 copy-start.36
  20.0 5.0 copy-start.32
  22.5 153.5 %all-reduce.8.cloned.1.call-start = ((), (), s32[]{:S(2)}) async-start(), calls=%async_computation.1 | async-start | bytes 4718592 | tf_op jit(solution)/shard_map/psum | solution.py:165
  81.2 0.7 copy-start.45
  81.2 211.3 %all-reduce.10.cloned.1.call-start = ((), (), s32[]{:S(2)}) async-start(), calls=%async_computation.2 | async-start | bytes 4718592 | tf_op jit(solution)/shard_map/psum | solution.py:191
  176.0 3.4 copy-start.2
  176.0 3.8 copy-start.9
  179.8 1.9 copy-start.47
  181.7 2.6 copy-start.30
  181.7 2.7 copy-start.46
  184.4 2.6 copy-start.28
  192.0 2.6 copy-start.49
  192.0 2.7 copy-start.51
  198.7 343.4 %all-reduce.14.cloned.1.call-start = ((), (), s32[]{:S(2)}) async-start(), calls=%async_computation.4 | async-start | bytes 9437184 | tf_op jit(solution)/shard_map/psum | solution.py:176
  292.5 5.0 copy-start.3
  292.5 5.0 copy-start.10
  292.5 5.2 copy-start.16
  297.7 5.7 copy-start.33
  301.2 2.1 copy-start.8
  316.6 4.2 copy-start.43
  321.2 1.9 copy-start.4
  323.1 1.1 copy-start.38
  325.6 2.5 copy-start.11
  328.9 1.1 copy-start.12
  328.9 2.1 copy-start.5
  331.6 1.4 copy-start.6
  333.0 3.8 copy-start.48
  335.5 29.7 %collective-permute-start = (f32[3,256,384]{1,2,0:T(8,128)}, f32[3,256,384]{1,2,0:T(8,128)}, u32[]{:S(2)}, u32[]{:S(2)}) collective-permute-start(f32[3,256,384]{1,2,0:T(8,128)} %dynamic-slice_select_fusion), channel_id=1, source_target_pairs={{4,0},{5,1},{6,2},{7,3},{12,8},{13,9},{14,10},{15,11},{20,16},{21,... | collective-permute-start | bytes 3538952 | tf_op jit(solution)/shard_map/while/body/eval_jaxpr/ppermute | solution.py:16
  336.8 3.9 copy-start.13
  336.8 3.9 copy-start.22
  336.8 3.8 copy-start.24
  348.0 17.3 %copy-start.7 = (f32[3,512,384]{1,2,0:T(8,128)S(1)}, f32[3,512,384]{1,2,0:T(8,128)}, u32[]{:S(2)}) copy-start(f32[3,512,384]{1,2,0:T(8,128)} %get-tuple-element.191) | copy-start | bytes 7077892
  366.7 1.0 copy-start.18
  366.8 1.5 copy-start.27
  368.2 1.1 copy-start.37
  371.6 492.1 %all-reduce.12.cloned.1.call-start = ((), (), s32[]{:S(2)}) async-start(), calls=%async_computation.3 | async-start | bytes 51904512 | tf_op jit(solution)/shard_map/psum | solution.py:308
  371.8 7.7 copy-start.31
  371.8 7.7 copy-start.52
  379.5 4.6 copy-start.50
  379.5 12.0 %slice-start = ((s8[4718592]{0:T(1024)(128)(4,1)}), s8[4194304]{0:T(1024)(128)(4,1)S(1)}, s32[]{:S(2)}) async-start(s8[4718592]{0:T(1024)(128)(4,1)} %bitcast.261), calls=%async_computation.5 | async-start | bytes 8388608
  384.1 4.6 copy-start.15
  384.1 4.6 copy-start.20
  384.1 7.4 slice-start.1
  388.6 2.8 copy-start.25
  391.5 2.6 copy-start.19
  397.4 144.7 %copy-start.40 = (f32[1536]{0:T(1024)S(1)}, f32[1536]{0:T(1024)}, u32[]{:S(2)}) copy-start(f32[1536]{0:T(1024)} %copy-done.39) | copy-start | bytes 18436
  863.6 3.4 copy-start.35
  863.6 4.4 copy-start.34
  867.0 2.3 copy-start.29
  868.0 4.3 copy-start.17
  869.3 6.2 slice-start.4
  872.4 3.4 slice-start.5
  872.4 7.0 slice-start.2
  875.8 4.6 slice-start.3
  (1 other events, 0.7 us)
Sparse Core Ops, SparseCore 0:
  22.7 29.8 all-gather.1
  81.3 94.6 all-reduce.7
  198.8 93.6 all-reduce.9
  371.7 170.3 all-reduce.13
  548.2 315.3 all-reduce.11
where the time goes:
time: 899 us; the launch traced here: 890 us
  waiting for transfers between devices  652 us (73%)
  matrix products  78 us (9%)
  local copies, waits for them, and re-layouts  66.8 us (7%)
  other arithmetic  49.9 us (6%)
  blocking collectives  25.9 us (3%)
  between operations  14.5 us (2%)
    psum x1, waiting for transfers between devices, on_device(): lax.psum((attn_gain_grad, query_grad, key_grad, value_grad, out_grad, ffn...  283 us
    psum x1, waiting for transfers between devices, on_device(): lax.psum(dot_wide(activated, w_down).astype(jnp.bfloat16), 'tensor')  144 us
    psum x1, waiting for transfers between devices, on_device(): lax.psum(dot_wide(attended, w_out).astype(jnp.bfloat16), 'tensor')  94.1 us
    psum x1, waiting for transfers between devices, on_device(): lax.psum((dot_wide(grad_gate, w_gate.T) + dot_wide(grad_up, w_up.T)).asty...  93.6 us
    dot_general x21, matrix products, dot_wide(): return jnp.dot(left_side, right_side, preferred_element_type=jnp.float32)  64.1 us
    unnamed x119, local copies, waits for them, and re-layouts  35.9 us
    psum x1, blocking collectives, on_device(): lax.psum((attn_gain_grad, query_grad, key_grad, value_grad, out_grad, ffn...  25.9 us
    all_gather x1, waiting for transfers between devices, on_device(): pair_all = lax.all_gather(pair_local, 'context', axis=1, tiled=True)  23.4 us
  transfers between devices with their start and end apart: 6, of which 6 were waited for; matrix products, arithmetic and copies ran while one was open for 7% of the time, Pallas kernels for 0%

commit v1 on v0

--- a/solution.py
+++ b/solution.py
@@ -173,9 +173,9 @@
     sigmoid_gate = jax.nn.sigmoid(gate_proj)
     silu_gate = gate_proj * sigmoid_gate
     activated = (silu_gate * up_proj).astype(brain_float_half)
-    ffn_total = lax.psum(dot_wide(activated, w_down).astype(jnp.bfloat16), "tensor").astype(
-        jnp.float32
-    )
+    ffn_total = jnp.sum(
+        lax.all_gather(dot_wide(activated, w_down).astype(jnp.bfloat16), "tensor"), axis=0
+    ).astype(jnp.float32)
     block_out = (
         (hidden_res + ffn_total).astype(brain_float_half).reshape(seq_count, slice_len, model_width)
     )

time: 899 us -> 988 us (1.099)
  waiting for transfers between devices: 652 us -> 744 us
  local copies, waits for them, and re-layouts: 66.8 us -> 56.8 us
    all_gather x0 -> x1, waiting for transfers between devices: none -> 164 us  [on_device(): lax.all_gather(dot_wide(activated, w_down).astype(jnp.bfloat16), 'tensor')]
    psum x1, waiting for transfers between devices: 144 us -> 70 us  [on_device(): lax.psum(back_attn.astype(jnp.bfloat16), 'tensor').astype(jnp.float32)]
    unnamed x119 -> x127, local copies, waits for them, and re-layouts: 35.9 us -> 36.3 us
  transfers between devices with their start and end apart: 6 -> 7, of which waited for: 6 -> 7; matrix products, arithmetic and copies ran while one was open for 7% -> 6% of each run, Pallas kernels for 0% -> 0%
where the time goes in v1:
time: 988 us; the launch traced here: 978 us
  waiting for transfers between devices  744 us (75%)
  matrix products  80.1 us (8%)
  local copies, waits for them, and re-layouts  56.8 us (6%)
  other arithmetic  53.3 us (5%)
  blocking collectives  25.9 us (3%)
  between operations  14.9 us (2%)
    psum x1, waiting for transfers between devices, on_device(): lax.psum((attn_gain_grad, query_grad, key_grad, value_grad, out_grad, ffn...  286 us
    all_gather x1, waiting for transfers between devices, on_device(): lax.all_gather(dot_wide(activated, w_down).astype(jnp.bfloat16), 'tensor')  164 us
    psum x1, waiting for transfers between devices, on_device(): lax.psum(dot_wide(attended, w_out).astype(jnp.bfloat16), 'tensor')  94.1 us
    psum x1, waiting for transfers between devices, on_device(): lax.psum((dot_wide(grad_gate, w_gate.T) + dot_wide(grad_up, w_up.T)).asty...  88.2 us
    psum x1, waiting for transfers between devices, on_device(): lax.psum(back_attn.astype(jnp.bfloat16), 'tensor').astype(jnp.float32)  70 us
    dot_general x21, matrix products, dot_wide(): return jnp.dot(left_side, right_side, preferred_element_type=jnp.float32)  64.8 us
    unnamed x127, local copies, waits for them, and re-layouts  36.3 us
    psum x1, blocking collectives, on_device(): lax.psum((attn_gain_grad, query_grad, key_grad, value_grad, out_grad, ffn...  25.9 us
  transfers between devices with their start and end apart: 7, of which 7 were waited for; matrix products, arithmetic and copies ran while one was open for 6% of the time, Pallas kernels for 0%

profile of v1, /device:TPU:0, one launch (start us, length us, event | category | flops | bytes accessed | tf_op | source)
XLA Modules:
  0.0 978.2 jit_solution(1336034903707998716)
XLA Ops:
  8.1 2.3 fusion.50
  10.4 2.3 fusion.52
  16.5 1.6 convolution_convert_fusion.3
  18.2 1.8 reshape.331
  20.0 2.5 pad_maximum_fusion
  22.6 2.4 copy.51
  25.0 3.1 fusion.57
  29.1 23.4 %all-gather.4.cloned.1.call-done = bf16[3,512,384]{1,0,2:T(4,128)(2,1)} async-done(((bf16[3,256,384]{1,0,2:T(4,128)(2,1)}), bf16[3,512,384]{1,0,2:T(4,128)(2,1)}) %all-gather.4.cloned.1.call-update) | async-done | bytes 1179664 | tf_op jit(solution)/shard_map/all_gather | solution.py:113
  52.6 2.7 copy.53
  55.3 5.6 while.42
  56.9 2.3 fusion.157
  59.3 1.6 select_reduce_fusion.2
  62.6 7.8 while.43
  63.1 2.4 fusion.162
  65.5 4.7 fusion.163
  70.4 3.3 copy.54
  73.7 3.3 reshape.332
  76.9 4.2 convolution_convert_fusion.1
  81.9 94.1 %all-reduce.7.cloned.1.call-done = bf16[768,1536]{1,0:T(8,128)(2,1)} async-done(((bf16[768,1536]{1,0:T(8,128)(2,1)}), bf16[768,1536]{1,0:T(8,128)(2,1)}) %all-reduce.7.cloned.1.call-update) | async-done | bytes 2359312 | tf_op jit(solution)/shard_map/psum | solution.py:165
  176.0 3.4 multiply_reduce_fusion
  181.7 2.6 fusion.70
  184.4 2.6 fusion.69
  187.0 5.0 multiply_convert_fusion.1
  192.0 2.6 fusion.71
  194.7 4.0 add_convert_fusion.1
  198.7 5.2 convolution_convert_fusion
  204.2 88.2 %all-reduce.9.cloned.1.call-done = bf16[768,1536]{1,0:T(8,128)(2,1)} async-done(((bf16[768,1536]{1,0:T(8,128)(2,1)}), bf16[768,1536]{1,0:T(8,128)(2,1)}) %all-reduce.9.cloned.1.call-update) | async-done | bytes 2359312 | tf_op jit(solution)/shard_map/psum | solution.py:191
  292.5 4.1 fusion.47
  296.6 163.7 %all-gather.6.cloned.1.call-done = bf16[3072,1536]{1,0:T(8,128)(2,1)} async-done(((bf16[768,1536]{1,0:T(8,128)(2,1)}), bf16[3072,1536]{1,0:T(8,128)(2,1)}) %all-gather.6.cloned.1.call-update) | async-done | bytes 9437200 | tf_op jit(solution)/shard_map/all_gather | solution.py:177
  460.3 7.2 reduce_sum.86
  467.5 6.8 fusion.44
  474.4 2.1 copy-done.13
  478.5 2.5 multiply_reduce_fusion.1
  481.0 1.7 copy.56
  484.2 1.7 broadcast_in_dim.84
  485.9 11.5 %while.44 = (s32[]{:T(128)}, f32[3,256,2,2,96]{1,4,3,2,0:T(8,128)}, f32[3,512,384]{1,2,0:T(8,128)}, s32[]{:T(128)}, s32[3,512]{1,0:T(4,128)S(1)}, /*index=5*/s32...) while((s32[]{:T(128)}, f32[3,256,2,2,96]{1,4,3,2,0:T(8,128)}, ...), condition=%wide.region_14.15_spmd.clone, body=%wide.region_13.14_spmd.clone.sunk | while | flops 1529643776 | bytes 85839216 | solution.py:248
  488.1 1.4 fusion.178
  489.5 2.4 fusion.176
  492.8 2.6 fusion.179
  497.5 2.5 dynamic-slice_select_fusion
  500.0 1.4 collective-permute-start
  501.4 6.0 fusion.77
  508.8 2.9 fusion.72
  511.8 18.4 %collective-permute-done = f32[3,256,384]{1,2,0:T(8,128)} collective-permute-done((f32[3,256,384]{1,2,0:T(8,128)}, f32[3,256,384]{1,2,0:T(8,128)}, u32[]{:S(2)}, u32[]{:S(2)}) %collective-permute-start) | collective-permute-done | bytes 1179680 | tf_op jit(solution)/shard_map/while/body/eval_jaxpr/ppermute | solution.py:16
  530.2 1.5 dynamic-slice_add_fusion
  534.3 2.2 add_convert_fusion
  536.7 1.4 copy-done.37
  538.2 6.4 fusion.76
  544.6 4.6 fusion.75
  549.2 2.8 fusion.74
  552.1 2.5 fusion.61
  554.6 1.6 convolution_bitcast_fusion.1
  556.2 1.6 fusion.78
  558.6 70.0 %all-reduce.11.cloned.1.call-done = bf16[768,1536]{1,0:T(8,128)(2,1)} async-done(((bf16[768,1536]{1,0:T(8,128)(2,1)}), bf16[768,1536]{1,0:T(8,128)(2,1)}) %all-reduce.11.cloned.1.call-update) | async-done | bytes 2359312 | tf_op jit(solution)/shard_map/psum | solution.py:299
  628.6 3.4 fusion.49
  632.0 25.9 %all-reduce = (f32[1536]{0:T(1024)}, f32[1536]{0:T(1024)}) all-reduce(f32[1536]{0:T(1024)S(1)} %get-tuple-element.347, f32[1536]{0:T(1024)S(1)} %get-tuple-element.345), channel_id=1, replica_groups=mesh['dp'=4,'context'=2,'tensor'=4] {'dp','context'}, use_global_device_ids=true, to_apply=%region_18.19 | all-reduce | flops 3072 | bytes 24576 | tf_op jit(solution)/shard_map/psum | solution.py:308
  657.8 6.0 fusion.41
  663.8 286.4 %all-reduce.13.cloned.1.call-done = (f32[1536,384]{1,0:T(8,128)}, f32[1536,192]{0,1:T(8,128)}, f32[1536,192]{0,1:T(8,128)}, f32[384,1536]{1,0:T(8,128)}, f32[153...) async-done(((f32[1536,384]{1,0:T(8,128)}, f32[1536,192]{0,1:T(8,128)}, f32[1536,192]{0,1:T(8,128)}, f32[384,1536]{1,0:T(8,128)}, f32[1536,1024]{1,0:T(8,128)}, ...) | async-done | bytes 25952272 | tf_op jit(solution)/shard_map/psum | solution.py:308
  950.2 3.4 copy.111
  955.9 1.4 copy.114
  957.3 1.6 copy-done.21
  958.9 3.2 copy.115
  962.4 3.2 copy.116
  967.0 3.2 copy.117
  (202 shorter events, 30.8 us)
Async XLA Ops:
  7.2 179.9 %copy-start = (bf16[1024,1536]{1,0:T(8,128)(2,1)S(1)}, bf16[1024,1536]{1,0:T(8,128)(2,1)}, u32[]{:S(2)}) copy-start(bf16[1024,1536]{1,0:T(8,128)(2,1)} %param.31) | copy-start | bytes 9437188
  7.2 3.2 copy-start.51
  7.2 45.4 %all-gather.4.cloned.1.call-start = ((), (), s32[]{:S(2)}) async-start(), calls=%async_computation | async-start | bytes 2359296 | tf_op jit(solution)/shard_map/all_gather | solution.py:113
  10.4 5.1 copy-start.48
  10.4 5.1 copy-start.46
  10.4 3.0 copy-start.33
  12.8 1.6 copy-start.17
  13.4 14.7 %copy-start.26 = (f32[3,256,48]{1,2,0:T(8,128)}, f32[3,256,48]{1,2,0:T(8,128)S(1)}, u32[]{:S(2)}) copy-start(f32[3,256,48]{1,2,0:T(8,128)S(1)} %get-tuple-element.437) | copy-start | bytes 442372
  13.4 14.7 %copy-start.28 = (f32[3,256,48]{1,2,0:T(8,128)}, f32[3,256,48]{1,2,0:T(8,128)S(1)}, u32[]{:S(2)}) copy-start(f32[3,256,48]{1,2,0:T(8,128)S(1)} %get-tuple-element.438) | copy-start | bytes 442372
  13.4 2.1 copy-start.4
  20.0 5.0 copy-start.39
  22.5 153.5 %all-reduce.7.cloned.1.call-start = ((), (), s32[]{:S(2)}) async-start(), calls=%async_computation.1 | async-start | bytes 4718592 | tf_op jit(solution)/shard_map/psum | solution.py:165
  81.2 211.3 %all-reduce.9.cloned.1.call-start = ((), (), s32[]{:S(2)}) async-start(), calls=%async_computation.2 | async-start | bytes 4718592 | tf_op jit(solution)/shard_map/psum | solution.py:191
  176.0 3.4 copy-start.5
  176.0 3.8 copy-start.19
  179.8 1.9 copy-start.54
  181.7 2.6 copy-start.36
  181.7 2.7 copy-start.53
  184.4 2.6 copy-start.31
  192.0 2.6 copy-start.55
  192.0 2.7 copy-start.57
  198.6 261.6 %all-gather.6.cloned.1.call-start = ((), (), s32[]{:S(2)}) async-start(), calls=%async_computation.4 | async-start | bytes 11796480 | tf_op jit(solution)/shard_map/all_gather | solution.py:177
  203.9 88.5 %copy-start.6 = (bf16[3,256,1536]{2,1,0:T(8,128)(2,1)S(1)}, bf16[3,256,1536]{2,1,0:T(8,128)(2,1)}, u32[]{:S(2)}) copy-start(bf16[3,256,1536]{2,1,0:T(8,128)(2,1)} %param.19) | copy-start | bytes 7077892
  204.0 424.6 %all-reduce.11.cloned.1.call-start = ((), (), s32[]{:S(2)}) async-start(), calls=%async_computation.3 | async-start | bytes 4718592 | tf_op jit(solution)/shard_map/psum | solution.py:299
  467.5 9.0 copy-start.40
  474.4 2.1 copy-start.13
  476.5 2.0 copy-start.20
  482.7 3.2 copy-start.2
  482.7 3.2 copy-start.8
  482.7 3.2 copy-start.50
  489.5 2.5 copy-start.14
  492.8 2.6 copy-start.15
  492.8 2.6 copy-start.10
  495.4 2.1 copy-start.3
  495.4 2.0 copy-start.9
  497.5 4.0 copy-start.32
  500.0 7.4 copy-start.16
  500.0 7.4 copy-start.27
  500.0 7.4 copy-start.29
  500.0 30.2 %collective-permute-start = (f32[3,256,384]{1,2,0:T(8,128)}, f32[3,256,384]{1,2,0:T(8,128)}, u32[]{:S(2)}, u32[]{:S(2)}) collective-permute-start(f32[3,256,384]{1,2,0:T(8,128)} %dynamic-slice_select_fusion), channel_id=1, source_target_pairs={{4,0},{5,1},{6,2},{7,3},{12,8},{13,9},{14,10},{15,11},{20,16},{21,... | collective-permute-start | bytes 3538952 | tf_op jit(solution)/shard_map/while/body/eval_jaxpr/ppermute | solution.py:16
  508.8 3.0 copy-start.24
  508.8 21.4 %copy-start.12 = (f32[3,512,384]{1,2,0:T(8,128)S(1)}, f32[3,512,384]{1,2,0:T(8,128)}, u32[]{:S(2)}) copy-start(f32[3,512,384]{1,2,0:T(8,128)} %get-tuple-element.798) | copy-start | bytes 7077892
  531.8 1.5 copy-start.34
  536.5 1.7 copy-start.37
  536.5 413.7 %all-reduce.13.cloned.1.call-start = ((), (), s32[]{:S(2)}) async-start(), calls=%async_computation.5 | async-start | bytes 51904512 | tf_op jit(solution)/shard_map/psum | solution.py:308
  538.2 6.4 copy-start.38
  538.2 6.4 copy-start.56
  538.2 13.9 %slice-start = ((s8[4718592]{0:T(1024)(128)(4,1)}), s8[4194304]{0:T(1024)(128)(4,1)S(1)}, s32[]{:S(2)}) async-start(s8[4718592]{0:T(1024)(128)(4,1)} %bitcast.262), calls=%async_computation.6 | async-start | bytes 8388608
  544.6 4.6 copy-start.18
  544.6 4.6 copy-start.25
  544.6 7.4 slice-start.1
  549.2 2.8 copy-start.30
  552.1 2.5 copy-start.23
  557.9 70.7 %copy-start.7 = (bf16[3,256,1536]{2,1,0:T(8,128)(2,1)S(1)}, bf16[3,256,1536]{2,1,0:T(8,128)(2,1)}, u32[]{:S(2)}) copy-start(bf16[3,256,1536]{2,1,0:T(8,128)(2,1)} %param.19) | copy-start | bytes 7077892
  557.9 70.7 %copy-start.47 = (f32[1536]{0:T(1024)S(1)}, f32[1536]{0:T(1024)}, u32[]{:S(2)}) copy-start(f32[1536]{0:T(1024)} %copy-done.46) | copy-start | bytes 18436
  950.2 3.4 copy-start.42
  950.2 4.4 copy-start.41
  953.6 2.3 copy-start.35
  954.6 4.3 copy-start.21
  955.9 6.2 slice-start.4
  958.9 3.4 slice-start.5
  958.9 7.0 slice-start.2
  962.4 4.6 slice-start.3
  967.0 4.2 copy-start.1
  (7 other events, 7.0 us)
Sparse Core Ops, SparseCore 0:
  22.7 29.8 all-gather.3
  81.3 94.6 all-reduce.6
  198.8 93.6 all-reduce.8
  294.5 165.7 all-gather.5
  536.6 91.8 all-reduce.10
  634.8 315.3 all-reduce.12
